TPU v7x, 32 devices: a whole 2x2x4 slice. The times are simulated.
32 devices in a mesh: row: 4 (over y, x), col: 8 (over z, core).
Axes of the slice: x: 2, y: 2, z: 4, core: 2. Of those that a mesh axis runs over, the one named last changes fastest.
Arguments:
- pair: float32 [256, 256, 128], P('row', 'col'), may hold values from -6 to 6
- valid_length: int32 [1], replicated, may hold values from 64 to 255
- tri_in: bfloat16 [128, 512], replicated, may hold values from -0.5 to 0.5
- tri_gate: bfloat16 [128, 128], replicated, may hold values from -0.5 to 0.5
- tri_out: bfloat16 [128, 128], replicated, may hold values from -0.5 to 0.5
- att_in: bfloat16 [128, 512], replicated, may hold values from -16.9705627 to 16.9705627
- att_bias: bfloat16 [128, 4], replicated, may hold values from -0.5 to 0.5
- att_out: bfloat16 [128, 128], replicated, may hold values from -0.5 to 0.5
Outputs:
- pair_out: float32 [256, 256, 128], P('row', 'col')
Inputs may be any that keep to these rules, and one draw needn't show every extreme that they name: Tokens at positions below valid_length[0] are real, the rest are padding.
All inputs are finite; a program needn't handle non-finite values.
Results may differ from a plain program's by a relative error of at most 0.025.
Values may be sent and summed in bfloat16 or wider, within the bound.
No kernel may reach another device: no remote copies, remote signals or barrier semaphores. Data moves between devices by JAX's collectives and lax.ppermute only.
A program may use at most 128 MiB of HBM per device.

v0:
```python
import jax
import jax.numpy as jnp
from jax import lax
from jax.sharding import PartitionSpec as P


def layer_norm(values):
    center = values - jnp.mean(values, axis=-1, keepdims=True)
    return center * lax.rsqrt(jnp.mean(center * center, axis=-1, keepdims=True) + 1e-05)


def fold_keys(carry, keys_piece, values_piece, query_blocks, bias_heads, mask_bias):
    count = keys_piece.shape[1]
    nblocks, brows, cols_dev, heads, head_size = query_blocks.shape
    key_blocks = keys_piece.reshape(nblocks, brows, count, heads, head_size)
    value_blocks = values_piece.reshape(nblocks, brows, count, heads, head_size)

    def one_block(packed):
        query, keys, values, run_max, run_sum, accum = packed
        scores = jnp.einsum("ijhd,ikhd->ihjk", query, keys, preferred_element_type=jnp.float32)
        scores = scores + bias_heads[None] + mask_bias[None, None, None, :]
        new_max = jnp.maximum(run_max, jnp.max(scores, axis=-1))
        factor = jnp.exp(run_max - new_max)
        expo = jnp.exp(scores - new_max[..., None])
        new_sum = run_sum * factor + jnp.sum(expo, axis=-1)
        new_acc = accum * jnp.transpose(factor, (0, 2, 1))[..., None]
        new_acc = new_acc + jnp.einsum("ihjk,ikhd->ijhd", expo, values.astype(jnp.float32))
        return (new_max, new_sum, new_acc)

    return lax.map(one_block, (query_blocks, key_blocks, value_blocks) + tuple(carry))


def per_device(pair, valid_length, tri_in, tri_gate, tri_out, att_in, att_bias, att_out):
    rows_dev, cols_dev, width = pair.shape
    hidden = tri_out.shape[0]
    heads = att_bias.shape[1]
    head_size = width // heads
    total = cols_dev * lax.axis_size("col")
    row_start = lax.axis_index("row") * rows_dev
    col_start = lax.axis_index("col") * cols_dev
    tokens = jnp.arange(total)
    keep_all = (tokens < valid_length[0]).astype(jnp.float32)
    keep_rows = lax.dynamic_slice_in_dim(keep_all, row_start, rows_dev)
    keep_cols = lax.dynamic_slice_in_dim(keep_all, col_start, cols_dev)
    normed_pair = layer_norm(pair).astype(jnp.bfloat16)
    projected = jnp.dot(normed_pair, tri_in, preferred_element_type=jnp.float32)
    weight = (keep_rows[:, None] * keep_cols[None, :])[:, :, None]
    left_edges = (
        jax.nn.sigmoid(projected[..., :hidden]) * projected[..., hidden : 2 * hidden] * weight
    ).astype(jnp.bfloat16)
    right_edges = (
        jax.nn.sigmoid(projected[..., 2 * hidden : 3 * hidden])
        * projected[..., 3 * hidden :]
        * weight
    ).astype(jnp.bfloat16)
    right_rows = lax.all_gather(right_edges, "row", axis=0, tiled=True)
    swapped = lax.psum_scatter(
        jnp.einsum(
            "jkc,ikc->jic", right_rows, left_edges, preferred_element_type=jnp.float32
        ).astype(jnp.bfloat16),
        "col",
        scatter_dimension=0,
        tiled=True,
    ).astype(jnp.float32)
    normed_swapped = layer_norm(swapped).astype(jnp.bfloat16)
    tri_part = jnp.einsum(
        "jic,cd->ijd", normed_swapped, tri_out, preferred_element_type=jnp.float32
    )
    middle = (
        pair
        + jax.nn.sigmoid(jnp.dot(normed_pair, tri_gate, preferred_element_type=jnp.float32))
        * tri_part
    )
    normed_mid = layer_norm(middle).astype(jnp.bfloat16)
    bias_local = jnp.dot(normed_mid, att_bias, preferred_element_type=jnp.float32).astype(
        jnp.bfloat16
    )
    bias_rows = lax.all_gather(bias_local, "row", axis=0, tiled=True)
    bias_cols = lax.all_to_all(bias_rows, "col", split_axis=0, concat_axis=1, tiled=True)
    bias_heads = jnp.transpose(bias_cols.astype(jnp.float32), (2, 0, 1))
    mask_bias = jnp.where(tokens < valid_length[0], 0.0, -1000000000.0).astype(jnp.float32)
    nblocks = rows_dev // 8
    query = (
        jnp.dot(normed_mid, att_in[:, :width], preferred_element_type=jnp.float32)
        * head_size ** (-0.5)
    ).astype(jnp.bfloat16)
    query_blocks = query.reshape(nblocks, 8, cols_dev, heads, head_size)
    gate = jax.nn.sigmoid(
        jnp.dot(normed_mid, att_in[:, 3 * width :], preferred_element_type=jnp.float32)
    )
    start_state = (
        jnp.full((nblocks, 8, heads, cols_dev), -1e30, jnp.float32),
        jnp.zeros((nblocks, 8, heads, cols_dev), jnp.float32),
        jnp.zeros((nblocks, 8, cols_dev, heads, head_size), jnp.float32),
    )
    made = jnp.dot(
        lax.all_gather(normed_mid, "col", axis=1, tiled=True),
        att_in[:, width : 3 * width],
        preferred_element_type=jnp.float32,
    )
    keys_piece = made[..., :width].astype(jnp.bfloat16)
    values_piece = made[..., width:].astype(jnp.bfloat16)
    state = fold_keys(start_state, keys_piece, values_piece, query_blocks, bias_heads, mask_bias)
    run_sum = state[1]
    accum = state[2]
    attended = accum / jnp.transpose(run_sum, (0, 1, 3, 2))[..., None]
    attended = attended.reshape(rows_dev, cols_dev, width)
    gated = (gate * attended).astype(jnp.bfloat16)
    return middle + jnp.dot(gated, att_out, preferred_element_type=jnp.float32)


def solution(mesh):
    placed = (P("row", "col", None), P(), P(), P(), P(), P(), P(), P())
    return jax.shard_map(
        per_device, mesh=mesh, in_specs=placed, out_specs=P("row", "col", None), check_vma=False
    )
```

profile of v0, /device:TPU:0, one launch (start us, length us, event | category | flops | bytes accessed | tf_op | source)
XLA Modules:
  0.0 237.1 jit_solution(12051169796513153194)
XLA Ops:
  7.4 1.6 reduce_sum.65
  9.0 1.9 multiply_reduce_fusion.1
  10.9 2.1 fusion.40
  13.0 1.4 fusion.31
  14.5 1.7 copy.17
  16.2 36.3 %all-gather.3.cloned.1.call-done = bf16[256,32,128]{2,1,0:T(8,128)(2,1)} async-done(((bf16[64,32,128]{2,1,0:T(8,128)(2,1)}), bf16[256,32,128]{2,1,0:T(8,128)(2,1)}) %all-gather.3.cloned.1.call-update) | async-done | bytes 2097168 | tf_op jit(solution)/shard_map/all_gather | solution.py:56
  52.5 3.9 %copy.18 = bf16[256,32,128]{0,1,2:T(8,128)(2,1)S(1)} copy(bf16[256,32,128]{2,1,0:T(8,128)(2,1)} %all-gather.3.cloned.1.call-done) | data formatting | bytes 4194304 | tf_op jit(solution)/shard_map/all_gather | solution.py:56
  56.4 3.3 %convert_bitcast_fusion = bf16[256,64,128]{0,1,2:T(8,128)(2,1)} fusion(bf16[64,32,128]{0,1,2:T(8,128)(2,1)S(1)} %copy.17, bf16[256,32,128]{0,1,2:T(8,128)(2,1)S(1)} %copy.18), kind=kOutput, calls=%fused_computation.24 | convolution fusion | flops 136314880 | bytes 6815744 | tf_op jit(solution)/shard_map/jkc,ikc->jic/dot_general | solution.py:58
  59.7 7.4 %copy.19 = bf16[256,64,128]{2,1,0:T(8,128)(2,1)} copy(bf16[256,64,128]{0,1,2:T(8,128)(2,1)} %convert_bitcast_fusion) | data formatting | bytes 8388608 | tf_op jit(solution)/shard_map/convert_element_type | solution.py:60
  67.1 50.0 %reduce-scatter.2.cloned.1.call-done = bf16[32,64,128]{2,1,0:T(8,128)(2,1)} async-done(((bf16[256,64,128]{2,1,0:T(8,128)(2,1)}), bf16[32,64,128]{2,1,0:T(8,128)(2,1)}) %reduce-scatter.2.cloned.1.call-update) | async-done | bytes 524304 | tf_op jit(solution)/shard_map/reduce_scatter | solution.py:57
  117.1 1.4 convert_reduce_fusion
  118.5 1.7 fusion.28
  120.2 1.6 fusion.29
  122.4 1.7 fusion.63
  124.1 0.6 multiply_reduce_fusion
  124.8 1.4 multiply_convert_fusion
  126.2 1.8 convolution_convert_fusion.1
  128.1 9.1 %all_gather.11 = bf16[256,32,4]{1,2,0:T(4,128)(2,1)S(1)} all-gather(bf16[64,32,4]{1,2,0:T(4,128)(2,1)S(1)} %convolution_convert_fusion.1), channel_id=1, replica_groups=mesh['row'=4,'col'=8] {'row'}, dimensions={0}, use_global_device_ids=true | all-gather | bytes 81920 | tf_op jit(solution)/shard_map/all_gather | solution.py:78
  137.2 0.9 reshape.132
  138.1 3.5 %all-to-all-start = ((bf16[8,2,2048]{2,1,0:T(2,128)(2,1)}), bf16[8,2,2048]{2,1,0:T(2,128)(2,1)S(1)}, u32[]{:S(2)}, u32[]{:S(2)}) async-start(bf16[8,2,2048]{2,1,0:T(2,128)(2,1)} %reshape.132), calls=%async_computation.1 | async-start | bytes 131072 | tf_op jit(solution)/shard_map/all_to_all | solution.py:79
  141.6 2.1 fusion.25
  143.7 3.1 %reshape.116 = bf16[8,8,32,4,32]{4,3,2,1,0:T(4,128)(2,1)S(1)} reshape(bf16[64,32,128]{2,1,0:T(8,128)(2,1)} %fusion.25) | data formatting | bytes 1048576 | tf_op jit(solution)/shard_map/reshape | solution.py:87
  146.9 2.2 all-to-all-done
  149.1 0.9 reshape.133
  150.0 1.0 convert_bitcast_fusion.1
  151.0 1.1 copy.22
  152.1 1.2 reshape.121
  153.3 19.8 %all-gather.5.cloned.1.call-done = bf16[64,256,128]{2,1,0:T(8,128)(2,1)} async-done(((bf16[64,32,128]{2,1,0:T(8,128)(2,1)}), bf16[64,256,128]{2,1,0:T(8,128)(2,1)}) %all-gather.5.cloned.1.call-update) | async-done | bytes 4194320 | tf_op jit(solution)/shard_map/all_gather | solution.py:97
  173.1 4.6 %convolution_convert_fusion = bf16[64,256,256]{1,2,0:T(8,128)(2,1)S(1)} fusion(bf16[64,256,128]{2,1,0:T(8,128)(2,1)} %all-gather.5.cloned.1.call-done, bf16[128,512]{1,0:T(8,128)(2,1)} %param.15), kind=kOutput, calls=%fused_computation.23 | convolution fusion | flops 1077936128 | bytes 12648448 | tf_op jit(solution)/shard_map/dot_general | solution.py:96
  177.7 3.5 %fusion.62 = (bf16[64,256,128]{1,2,0:T(8,128)(2,1)}, bf16[64,256,128]{1,2,0:T(8,128)(2,1)}) fusion(bf16[64,256,256]{1,2,0:T(8,128)(2,1)S(1)} %convolution_convert_fusion), kind=kLoop, calls=%fused_computation.96 | loop fusion | bytes 16777216 | tf_op jit(solution)/shard_map/slice | solution.py:102
  181.2 39.1 %while.13 = (s32[]{:T(128)}, f32[8,8,4,32]{3,2,1,0:T(4,128)S(1)}, f32[8,8,32,4,32]{2,4,3,1,0:T(8,128)}, bf16[8,8,32,4,32]{4,3,2,1,0:T(4,128)(2,1)S(1)}, bf16[8,8...) while((s32[]{:T(128)}, f32[8,8,4,32]{3,2,1,0:T(4,128)S(1)}, ...), condition=%wide.region_10.11_spmd.clone, body=%wide.region_7.10_spmd.clone.sunk | while | flops 35165696 | bytes 5131381 | solution.py:30
  181.2 0.6 compare_select_fusion.2
  182.0 1.4 fusion.76
  183.4 0.4 fusion.78
  183.8 2.3 fusion.79
  186.1 0.6 compare_select_fusion.2
  186.9 1.4 fusion.76
  188.3 0.4 fusion.78
  188.8 2.3 fusion.79
  191.1 0.6 compare_select_fusion.2
  191.8 1.4 fusion.76
  193.3 0.4 fusion.78
  193.7 2.2 fusion.79
  195.9 0.6 compare_select_fusion.2
  196.7 1.4 fusion.76
  198.1 0.4 fusion.78
  198.6 2.2 fusion.79
  200.8 0.6 compare_select_fusion.2
  201.5 1.4 fusion.76
  203.0 0.4 fusion.78
  203.4 2.2 fusion.79
  205.7 0.6 compare_select_fusion.2
  206.5 1.4 fusion.76
  207.9 0.4 fusion.78
  208.3 2.2 fusion.79
  210.6 0.6 compare_select_fusion.2
  211.3 1.4 fusion.76
  213.2 2.2 fusion.79
  215.4 0.6 compare_select_fusion.2
  216.2 1.4 fusion.76
  218.1 2.2 fusion.79
  220.3 5.0 %broadcast_divide_fusion = f32[8,8,32,4,32]{2,4,3,1,0:T(8,128)} fusion(f32[8,8,32,4,32]{2,4,3,1,0:T(8,128)} %get-tuple-element.48, f32[8,8,32,4]{2,3,1,0:T(4,128)S(1)} %bitcast.104), kind=kLoop, calls=%fused_computation.25 | loop fusion | flops 262144 | bytes 2129920 | tf_op jit(solution)/shard_map/div | solution.py:106
  225.4 2.9 %copy.27 = f32[64,32,128]{2,1,0:T(8,128)S(1)} copy(f32[64,32,128]{1,2,0:T(8,128)} %bitcast.98) | data formatting | bytes 2097152 | tf_op jit(solution)/shard_map/reshape | solution.py:107
  228.2 2.3 convolution_add_fusion.1
  (59 shorter events, 2.9 us)
Async XLA Ops:
  6.5 4.4 %copy-start = (bf16[128,512]{1,0:T(8,128)(2,1)S(1)}, bf16[128,512]{1,0:T(8,128)(2,1)}, u32[]{:S(2)}) copy-start(bf16[128,512]{1,0:T(8,128)(2,1)} %param.12) | copy-start | bytes 393220
  6.5 45.9 %all-gather.3.cloned.1.call-start = ((), (), s32[]{:S(2)}) async-start(), calls=%async_computation.2 | async-start | bytes 2621440 | tf_op jit(solution)/shard_map/all_gather | solution.py:56
  14.4 102.7 %reduce-scatter.2.cloned.1.call-start = ((), (), s32[]{:S(2)}) async-start(), calls=%async_computation.3 | async-start | bytes 4718592 | tf_op jit(solution)/shard_map/reduce_scatter | solution.py:57
  67.1 54.9 %copy-start.3 = (bf16[128,128]{1,0:T(8,128)(2,1)S(1)}, bf16[128,128]{1,0:T(8,128)(2,1)}, u32[]{:S(2)}) copy-start(bf16[128,128]{1,0:T(8,128)(2,1)} %param.14) | copy-start | bytes 98308
  67.1 55.3 %copy-start.1 = (f32[64,32,128]{2,1,0:T(8,128)S(1)}, f32[64,32,128]{2,1,0:T(8,128)}, u32[]{:S(2)}) copy-start(f32[64,32,128]{2,1,0:T(8,128)} %param.10) | copy-start | bytes 3145732
  67.1 55.3 %copy-start.5 = (bf16[128,128]{1,0:T(8,128)(2,1)S(1)}, bf16[128,128]{1,0:T(8,128)(2,1)}, u32[]{:S(2)}) copy-start(bf16[128,128]{1,0:T(8,128)(2,1)} %param.13) | copy-start | bytes 98308
  67.1 106.0 %all-gather.5.cloned.1.call-start = ((), (), s32[]{:S(2)}) async-start(), calls=%async_computation.4 | async-start | bytes 4718592 | tf_op jit(solution)/shard_map/all_gather | solution.py:97
  122.3 3.9 %copy-start.4 = (bf16[128,4]{0,1:T(4,128)(2,1)S(1)}, bf16[128,4]{0,1:T(4,128)(2,1)}, u32[]{:S(2)}) copy-start(bf16[128,4]{0,1:T(4,128)(2,1)} %param.16) | copy-start | bytes 3076
  138.1 11.0 %all-to-all-start = ((bf16[8,2,2048]{2,1,0:T(2,128)(2,1)}), bf16[8,2,2048]{2,1,0:T(2,128)(2,1)S(1)}, u32[]{:S(2)}, u32[]{:S(2)}) async-start(bf16[8,2,2048]{2,1,0:T(2,128)(2,1)} %reshape.132), calls=%async_computation.1 | async-start | bytes 131072 | tf_op jit(solution)/shard_map/all_to_all | solution.py:79
  225.4 2.9 %copy-start.2 = (bf16[64,32,128]{2,1,0:T(8,128)(2,1)S(1)}, bf16[64,32,128]{2,1,0:T(8,128)(2,1)}, u32[]{:S(2)}) copy-start(bf16[64,32,128]{2,1,0:T(8,128)(2,1)} %multiply_convert_fusion) | copy-start | bytes 1572868
  225.4 2.9 %copy-start.6 = (bf16[128,128]{1,0:T(8,128)(2,1)S(1)}, bf16[128,128]{1,0:T(8,128)(2,1)}, u32[]{:S(2)}) copy-start(bf16[128,128]{1,0:T(8,128)(2,1)} %param.17) | copy-start | bytes 98308
Sparse Core Ops, SparseCore 0:
  14.5 37.8 all-gather.2
  67.2 49.8 reduce-scatter.1
  126.3 46.7 all-gather.4
where the time goes:
time: 239 us; the launch traced here: 237 us
  waiting for transfers between devices  108 us (45%)
  matrix products  47.5 us (20%)
  local copies, waits for them, and re-layouts  27.6 us (12%)
  other arithmetic  26.6 us (11%)
  between operations  14 us (6%)
  blocking collectives  9.12 us (4%)
  starting transfers between devices  3.61 us (2%)
    reduce_scatter x1, waiting for transfers between devices, per_device(): lax.psum_scatter(jnp.einsum('jkc,ikc->jic', right_rows, left_edges, prefe...  50 us
    all_gather x1, waiting for transfers between devices, per_device(): right_rows = lax.all_gather(right_edges, 'row', axis=0, tiled=True)  36.3 us
    all_gather x1, waiting for transfers between devices, per_device(): lax.all_gather(normed_mid, 'col', axis=1, tiled=True)  19.8 us
    dot_general x8, matrix products, one_block(): jnp.einsum('ihjk,ikhd->ijhd', expo, values.astype(jnp.float32))  17.9 us
    dot_general x8, matrix products, one_block(): jnp.einsum('ijhd,ikhd->ihjk', query, keys, preferred_element_type=jnp.flo...  11.3 us
    all_gather x1, blocking collectives, per_device(): bias_rows = lax.all_gather(bias_local, 'row', axis=0, tiled=True)  9.12 us
    convert_element_type x1, local copies, waits for them, and re-layouts, per_device(): swapped = lax.psum_scatter(jnp.einsum('jkc,ikc->jic', right_rows, left_ed...  7.38 us
    select_n x8, other arithmetic, per_device(): jnp.where(tokens < valid_length[0], 0.0, -1000000000.0).astype(jnp.float32)  5.17 us
  transfers between devices with their start and end apart: 4, of which 4 were waited for; matrix products, arithmetic and copies ran while one was open for 6% of the time, Pallas kernels for 0%

commit v1 on v0

--- a/solution.py
+++ b/solution.py
@@ -2,6 +2,29 @@
 import jax.numpy as jnp
 from jax import lax
 from jax.sharding import PartitionSpec as P
+
+
+def measure_plate(array_in, a0):
+    oldest = lax.axis_size("row")
+    o_now = lax.axis_index("row")
+    b_next, v1, z_new = (oldest, o_now, array_in.shape[0])
+    p_next, all_values = ([], [])
+    h_now = newest = array_in
+    for nth in range(b_next // 2 + 1):
+        tile_out = a0(h_now, (v1 - nth) % b_next * z_new)
+        p_next.append(tile_out)
+        if 0 < nth < b_next - b_next // 2:
+            main = a0(newest, (v1 + nth) % b_next * z_new)
+            all_values.append(main)
+        h_now = lax.ppermute(
+            h_now, axis_name="row", perm=[(ii, (ii + 1) % b_next) for ii in range(b_next)]
+        )
+        newest = lax.ppermute(
+            newest, axis_name="row", perm=[(ii, (ii - 1) % b_next) for ii in range(b_next)]
+        )
+    earlier = jnp.concatenate([*p_next[::-1], *all_values], axis=0)
+    near = jnp.roll(earlier, (v1 - b_next // 2) * p_next[0].shape[0], axis=0)
+    return near
 
 
 def layer_norm(values):
@@ -53,10 +76,12 @@
         * projected[..., 3 * hidden :]
         * weight
     ).astype(jnp.bfloat16)
-    right_rows = lax.all_gather(right_edges, "row", axis=0, tiled=True)
     swapped = lax.psum_scatter(
-        jnp.einsum(
-            "jkc,ikc->jic", right_rows, left_edges, preferred_element_type=jnp.float32
+        measure_plate(
+            right_edges,
+            lambda part, start: jnp.einsum(
+                "jkc,ikc->jic", part, left_edges, preferred_element_type=jnp.float32
+            ),
         ).astype(jnp.bfloat16),
         "col",
         scatter_dimension=0,

time: 239 us -> 268 us (1.12)
  local copies, waits for them, and re-layouts: 27.6 us -> 64.1 us
  waiting for transfers between devices: 108 us -> 87.5 us
  matrix products: 47.5 us -> 55 us
  starting transfers between devices: 3.61 us -> 8.61 us
    all_gather x1 -> x0, waiting for transfers between devices: 36.3 us -> none  [per_device(): right_rows = lax.all_gather(right_edges, 'row', axis=0, tiled=True)]
    concatenate x0 -> x1, local copies, waits for them, and re-layouts: none -> 19.4 us  [measure_plate(): near = jnp.roll(earlier, (v1 - b_next // 2) * p_next[0].shape[0], axis=0)]
    ppermute x0 -> x3, waiting for transfers between devices: none -> 13.2 us  [the longest x1 6.98 us: measure_plate(): lax.ppermute(newest, axis_name='row', perm=[(ii, (ii - 1) % b_next) for i...]
    ppermute x0 -> x3, local copies, waits for them, and re-layouts: none -> 11.1 us  [the longest x2 7.41 us: measure_plate(): lax.ppermute(h_now, axis_name='row', perm=[(ii, (ii + 1) % b_next) for ii...]
    convert_element_type x1 -> x3, local copies, waits for them, and re-layouts: 7.38 us -> 18 us  [the longest x2 14.3 us: per_device(): swapped = lax.psum_scatter(measure_plate(right_edges, lambda part, start:...]
    dot_general x1 -> x4, matrix products: 3.28 us -> 10.8 us  [per_device(): jnp.einsum('jkc,ikc->jic', part, left_edges, preferred_element_type=jnp.f...]
    ppermute x0 -> x3, starting transfers between devices: none -> 4.99 us  [the longest x2 4.02 us: measure_plate(): lax.ppermute(h_now, axis_name='row', perm=[(ii, (ii + 1) % b_next) for ii...]
    all_gather x1 -> x0, local copies, waits for them, and re-layouts: 3.91 us -> none  [per_device(): right_rows = lax.all_gather(right_edges, 'row', axis=0, tiled=True)]
  transfers between devices with their start and end apart: 4 -> 6, of which waited for: 4 -> 6; matrix products, arithmetic and copies ran while one was open for 6% -> 12% of each run, Pallas kernels for 0% -> 0%
where the time goes in v1:
time: 268 us; the launch traced here: 265 us
  waiting for transfers between devices  87.5 us (33%)
  local copies, waits for them, and re-layouts  64.1 us (24%)
  matrix products  55 us (21%)
  other arithmetic  25.6 us (10%)
  between operations  14.4 us (5%)
  blocking collectives  9.12 us (3%)
  starting transfers between devices  8.61 us (3%)
    reduce_scatter x1, waiting for transfers between devices, per_device(): lax.psum_scatter(measure_plate(right_edges, lambda part, start: jnp.einsu...  50.3 us
    all_gather x1, waiting for transfers between devices, per_device(): lax.all_gather(normed_mid, 'col', axis=1, tiled=True)  21.4 us
    concatenate x1, local copies, waits for them, and re-layouts, measure_plate(): near = jnp.roll(earlier, (v1 - b_next // 2) * p_next[0].shape[0], axis=0)  19.4 us
    dot_general x8, matrix products, one_block(): jnp.einsum('ihjk,ikhd->ijhd', expo, values.astype(jnp.float32))  17.9 us
    convert_element_type x2, local copies, waits for them, and re-layouts, per_device(): swapped = lax.psum_scatter(measure_plate(right_edges, lambda part, start:...  14.3 us
    dot_general x8, matrix products, one_block(): jnp.einsum('ijhd,ikhd->ihjk', query, keys, preferred_element_type=jnp.flo...  11.3 us
    dot_general x4, matrix products, per_device(): jnp.einsum('jkc,ikc->jic', part, left_edges, preferred_element_type=jnp.f...  10.8 us
    all_gather x1, blocking collectives, per_device(): bias_rows = lax.all_gather(bias_local, 'row', axis=0, tiled=True)  9.12 us
  transfers between devices with their start and end apart: 6, of which 6 were waited for; matrix products, arithmetic and copies ran while one was open for 12% of the time, Pallas kernels for 0%

profile of v1, /device:TPU:0, one launch (start us, length us, event | category | flops | bytes accessed | tf_op | source)
XLA Modules:
  0.0 264.6 jit_solution(12739983495630724554)
XLA Ops:
  7.4 1.6 reduce_sum.65
  9.0 1.9 multiply_reduce_fusion.1
  10.9 2.1 fusion.40
  13.0 1.4 fusion.31
  14.4 3.0 %collective-permute-start = (bf16[64,32,128]{2,1,0:T(8,128)(2,1)}, bf16[64,32,128]{2,1,0:T(8,128)(2,1)}, u32[]{:S(2)}, u32[]{:S(2)}) collective-permute-start(bf16[64,32,128]{2,1,0:T(8,128)(2,1)} %get-tuple-element.107), channel_id=1, source_target_pairs={{0,8},{8,16},{16,24},{24,0},{1,9},{9,17},{17,25},{25,1},{2,10},{10... | collective-permute-start | bytes 1572872 | tf_op jit(solution)/shard_map/ppermute | solution.py:19
  17.3 1.0 collective-permute-start.2
  18.3 3.7 %copy.28 = bf16[64,32,128]{0,1,2:T(8,128)(2,1)} copy(bf16[64,32,128]{2,1,0:T(8,128)(2,1)} %get-tuple-element.107) | data formatting | bytes 1048576 | tf_op jit(solution)/shard_map/convert_element_type | solution.py:78
  22.0 1.7 copy.23
  23.8 2.0 convolution_bitcast_fusion.2
  25.7 5.7 %collective-permute-done = bf16[64,32,128]{2,1,0:T(8,128)(2,1)} collective-permute-done((bf16[64,32,128]{2,1,0:T(8,128)(2,1)}, bf16[64,32,128]{2,1,0:T(8,128)(2,1)}, u32[]{:S(2)}, u32[]{:S(2)}) %collective-permute-start) | collective-permute-done | bytes 524320 | tf_op jit(solution)/shard_map/ppermute | solution.py:19
  31.4 1.1 collective-permute-start.1
  32.5 3.7 %copy.26 = bf16[64,32,128]{0,1,2:T(8,128)(2,1)} copy(bf16[64,32,128]{2,1,0:T(8,128)(2,1)} %collective-permute-done) | data formatting | bytes 1048576 | tf_op jit(solution)/shard_map/ppermute | solution.py:19
  36.2 7.0 %collective-permute-done.2 = bf16[64,32,128]{2,1,0:T(8,128)(2,1)} collective-permute-done((bf16[64,32,128]{2,1,0:T(8,128)(2,1)}, bf16[64,32,128]{2,1,0:T(8,128)(2,1)}, u32[]{:S(2)}, u32[]{:S(2)}) %collective-permute-start.2) | collective-permute-done | bytes 524320 | tf_op jit(solution)/shard_map/ppermute | solution.py:22
  43.2 3.7 %copy.30 = bf16[64,32,128]{0,1,2:T(8,128)(2,1)} copy(bf16[64,32,128]{2,1,0:T(8,128)(2,1)} %collective-permute-done.2) | data formatting | bytes 1048576 | tf_op jit(solution)/shard_map/ppermute | solution.py:22
  46.9 3.5 %convolution_bitcast_fusion.3 = bf16[64,64,128]{0,1,2:T(8,128)(2,1)} fusion(bf16[64,32,128]{0,1,2:T(8,128)(2,1)S(1)} %copy.23, bf16[64,32,128]{0,1,2:T(8,128)(2,1)} %copy.26), kind=kOutput, calls=%fused_computation.27 | convolution fusion | flops 33554432 | bytes 2097152 | tf_op jit(solution)/shard_map/jkc,ikc->jic/dot_general | solution.py:82
  50.3 2.1 convolution_bitcast_fusion.1
  53.0 3.7 %copy.24 = bf16[64,32,128]{0,1,2:T(8,128)(2,1)} copy(bf16[64,32,128]{2,1,0:T(8,128)(2,1)} %collective-permute-done.1) | data formatting | bytes 1048576 | tf_op jit(solution)/shard_map/ppermute | solution.py:19
  56.7 3.3 %convolution_bitcast_fusion.4 = bf16[64,64,128]{0,1,2:T(8,128)(2,1)} fusion(bf16[64,32,128]{0,1,2:T(8,128)(2,1)S(1)} %copy.23, bf16[64,32,128]{0,1,2:T(8,128)(2,1)} %copy.24), kind=kOutput, calls=%fused_computation.28 | convolution fusion | flops 33554432 | bytes 2097152 | tf_op jit(solution)/shard_map/jkc,ikc->jic/dot_general | solution.py:82
  60.0 19.4 %concatenate.6 = bf16[512,64,128]{0,1,2:T(8,128)(2,1)} concatenate(bf16[64,64,128]{0,1,2:T(8,128)(2,1)} %convolution_bitcast_fusion.4, bf16[64,64,128]{0,1,2:T(8,128)(2,1)} %convolution_bitcast_fusion.3, bf16[64,64,128]{0,1,2:T(8,128)(2,1)S(1)} %convolution_bitcast_fusion.2, bf16[64,64,128]{0,1,2:T(8,128)(2,1)} %convolution_bitcast_fusion.1, ...), dimensions={0} | concatenate | bytes 16777216 | tf_op jit(solution)/shard_map/jit(_roll_dynamic)/concatenate | solution.py:26
  79.4 7.0 %dynamic-slice_convert_fusion = bf16[256,64,128]{0,1,2:T(8,128)(2,1)} fusion(bf16[512,64,128]{0,1,2:T(8,128)(2,1)} %concatenate.6, s32[]{:T(128)S(6)} %select_n.26), kind=kLoop, calls=%fused_computation.23 | loop fusion | bytes 8388612 | tf_op jit(solution)/shard_map/convert_element_type | solution.py:85
  86.3 7.4 %copy.31 = bf16[256,64,128]{2,1,0:T(8,128)(2,1)} copy(bf16[256,64,128]{0,1,2:T(8,128)(2,1)} %dynamic-slice_convert_fusion) | data formatting | bytes 8388608 | tf_op jit(solution)/shard_map/convert_element_type | solution.py:85
  94.0 50.3 %reduce-scatter.2.cloned.1.call-done = bf16[32,64,128]{2,1,0:T(8,128)(2,1)} async-done(((bf16[256,64,128]{2,1,0:T(8,128)(2,1)}), bf16[32,64,128]{2,1,0:T(8,128)(2,1)}) %reduce-scatter.2.cloned.1.call-update) | async-done | bytes 524304 | tf_op jit(solution)/shard_map/reduce_scatter | solution.py:79
  144.4 1.4 convert_reduce_fusion
  145.8 1.7 fusion.28
  147.5 1.6 fusion.29
  149.6 1.7 fusion.63
  152.0 1.4 multiply_convert_fusion
  153.4 1.8 convolution_convert_fusion.1
  155.3 9.1 %all_gather.7 = bf16[256,32,4]{1,2,0:T(4,128)(2,1)S(1)} all-gather(bf16[64,32,4]{1,2,0:T(4,128)(2,1)S(1)} %convolution_convert_fusion.1), channel_id=1, replica_groups=mesh['row'=4,'col'=8] {'row'}, dimensions={0}, use_global_device_ids=true | all-gather | bytes 81920 | tf_op jit(solution)/shard_map/all_gather | solution.py:103
  164.4 0.9 reshape.132
  165.3 3.3 %all-to-all-start = ((bf16[8,2,2048]{2,1,0:T(2,128)(2,1)}), bf16[8,2,2048]{2,1,0:T(2,128)(2,1)S(1)}, u32[]{:S(2)}, u32[]{:S(2)}) async-start(bf16[8,2,2048]{2,1,0:T(2,128)(2,1)} %reshape.132), calls=%async_computation.1 | async-start | bytes 131072 | tf_op jit(solution)/shard_map/all_to_all | solution.py:104
  168.7 2.1 fusion.25
  170.8 3.1 %reshape.116 = bf16[8,8,32,4,32]{4,3,2,1,0:T(4,128)(2,1)S(1)} reshape(bf16[64,32,128]{2,1,0:T(8,128)(2,1)} %fusion.25) | data formatting | bytes 1048576 | tf_op jit(solution)/shard_map/reshape | solution.py:112
  173.9 2.4 all-to-all-done
  176.5 1.1 copy.34
  177.6 1.2 reshape.121
  178.8 21.4 %all-gather.2.cloned.1.call-done = bf16[64,256,128]{2,1,0:T(8,128)(2,1)} async-done(((bf16[64,32,128]{2,1,0:T(8,128)(2,1)}), bf16[64,256,128]{2,1,0:T(8,128)(2,1)}) %all-gather.2.cloned.1.call-update) | async-done | bytes 4194320 | tf_op jit(solution)/shard_map/all_gather | solution.py:122
  200.3 4.6 %convolution_convert_fusion = bf16[64,256,256]{1,2,0:T(8,128)(2,1)S(1)} fusion(bf16[64,256,128]{2,1,0:T(8,128)(2,1)} %all-gather.2.cloned.1.call-done, bf16[128,512]{1,0:T(8,128)(2,1)} %param.15), kind=kOutput, calls=%fused_computation.24 | convolution fusion | flops 1077936128 | bytes 12648448 | tf_op jit(solution)/shard_map/dot_general | solution.py:121
  204.9 3.5 %fusion.62 = (bf16[64,256,128]{1,2,0:T(8,128)(2,1)}, bf16[64,256,128]{1,2,0:T(8,128)(2,1)}) fusion(bf16[64,256,256]{1,2,0:T(8,128)(2,1)S(1)} %convolution_convert_fusion), kind=kLoop, calls=%fused_computation.100 | loop fusion | bytes 16777216 | tf_op jit(solution)/shard_map/slice | solution.py:127
  208.4 39.1 %while.13 = (s32[]{:T(128)}, f32[8,8,4,32]{3,2,1,0:T(4,128)S(1)}, f32[8,8,32,4,32]{2,4,3,1,0:T(8,128)}, bf16[8,8,32,4,32]{4,3,2,1,0:T(4,128)(2,1)S(1)}, bf16[8,8...) while((s32[]{:T(128)}, f32[8,8,4,32]{3,2,1,0:T(4,128)S(1)}, ...), condition=%wide.region_10.11_spmd.clone, body=%wide.region_7.10_spmd.clone.sunk | while | flops 35165696 | bytes 5131381 | solution.py:53
  208.4 0.6 compare_select_fusion.2
  209.1 1.4 fusion.82
  211.0 2.3 fusion.85
  213.3 0.6 compare_select_fusion.2
  214.1 1.4 fusion.82
  215.9 2.3 fusion.85
  218.2 0.6 compare_select_fusion.2
  219.0 1.4 fusion.82
  220.9 2.2 fusion.85
  223.1 0.6 compare_select_fusion.2
  223.9 1.4 fusion.82
  225.8 2.2 fusion.85
  228.7 1.4 fusion.82
  230.6 2.3 fusion.85
  232.9 0.6 compare_select_fusion.2
  233.6 1.4 fusion.82
  235.5 2.2 fusion.85
  238.5 1.4 fusion.82
  240.4 2.2 fusion.85
  243.4 1.4 fusion.82
  245.3 2.2 fusion.85
  247.5 5.0 %broadcast_divide_fusion = f32[8,8,32,4,32]{2,4,3,1,0:T(8,128)} fusion(f32[8,8,32,4,32]{2,4,3,1,0:T(8,128)} %get-tuple-element.48, f32[8,8,32,4]{2,3,1,0:T(4,128)S(1)} %bitcast.116), kind=kLoop, calls=%fused_computation.29 | loop fusion | flops 262144 | bytes 2129920 | tf_op jit(solution)/shard_map/div | solution.py:131
  252.6 2.9 %copy.39 = f32[64,32,128]{2,1,0:T(8,128)S(1)} copy(f32[64,32,128]{1,2,0:T(8,128)} %bitcast.110) | data formatting | bytes 2097152 | tf_op jit(solution)/shard_map/reshape | solution.py:132
  255.4 2.3 convolution_add_fusion.1
  (76 shorter events, 8.9 us)
Async XLA Ops:
  6.5 4.4 %copy-start = (bf16[128,512]{1,0:T(8,128)(2,1)S(1)}, bf16[128,512]{1,0:T(8,128)(2,1)}, u32[]{:S(2)}) copy-start(bf16[128,512]{1,0:T(8,128)(2,1)} %param.12) | copy-start | bytes 393220
  6.5 137.8 %reduce-scatter.2.cloned.1.call-start = ((), (), s32[]{:S(2)}) async-start(), calls=%async_computation.2 | async-start | bytes 4718592 | tf_op jit(solution)/shard_map/reduce_scatter | solution.py:79
  14.4 17.0 %collective-permute-start = (bf16[64,32,128]{2,1,0:T(8,128)(2,1)}, bf16[64,32,128]{2,1,0:T(8,128)(2,1)}, u32[]{:S(2)}, u32[]{:S(2)}) collective-permute-start(bf16[64,32,128]{2,1,0:T(8,128)(2,1)} %get-tuple-element.107), channel_id=1, source_target_pairs={{0,8},{8,16},{16,24},{24,0},{1,9},{9,17},{17,25},{25,1},{2,10},{10... | collective-permute-start | bytes 1572872 | tf_op jit(solution)/shard_map/ppermute | solution.py:19
  17.3 25.8 %collective-permute-start.2 = (bf16[64,32,128]{2,1,0:T(8,128)(2,1)}, bf16[64,32,128]{2,1,0:T(8,128)(2,1)}, u32[]{:S(2)}, u32[]{:S(2)}) collective-permute-start(bf16[64,32,128]{2,1,0:T(8,128)(2,1)} %get-tuple-element.107), channel_id=1, source_target_pairs={{0,24},{8,0},{16,8},{24,16},{1,25},{9,1},{17,9},{25,17},{2,26},{10... | collective-permute-start | bytes 1572872 | tf_op jit(solution)/shard_map/ppermute | solution.py:22
  31.4 21.6 %collective-permute-start.1 = (bf16[64,32,128]{2,1,0:T(8,128)(2,1)}, bf16[64,32,128]{2,1,0:T(8,128)(2,1)}, u32[]{:S(2)}, u32[]{:S(2)}) collective-permute-start(bf16[64,32,128]{2,1,0:T(8,128)(2,1)} %collective-permute-done), channel_id=1, source_target_pairs={{0,8},{8,16},{16,24},{24,0},{1,9},{9,17},{17,25},{25,1},{2,10},{10... | collective-permute-start | bytes 1572872 | tf_op jit(solution)/shard_map/ppermute | solution.py:19
  46.9 3.5 %copy-start.4 = (bf16[64,32,128]{0,1,2:T(8,128)(2,1)S(1)}, bf16[64,32,128]{0,1,2:T(8,128)(2,1)}, u32[]{:S(2)}) copy-start(bf16[64,32,128]{0,1,2:T(8,128)(2,1)} %copy.30) | copy-start | bytes 1572868
  93.7 55.4 %copy-start.6 = (bf16[128,128]{1,0:T(8,128)(2,1)S(1)}, bf16[128,128]{1,0:T(8,128)(2,1)}, u32[]{:S(2)}) copy-start(bf16[128,128]{1,0:T(8,128)(2,1)} %param.14) | copy-start | bytes 98308
  93.7 55.8 %copy-start.2 = (f32[64,32,128]{2,1,0:T(8,128)S(1)}, f32[64,32,128]{2,1,0:T(8,128)}, u32[]{:S(2)}) copy-start(f32[64,32,128]{2,1,0:T(8,128)} %param.10) | copy-start | bytes 3145732
  93.7 55.8 %copy-start.8 = (bf16[128,128]{1,0:T(8,128)(2,1)S(1)}, bf16[128,128]{1,0:T(8,128)(2,1)}, u32[]{:S(2)}) copy-start(bf16[128,128]{1,0:T(8,128)(2,1)} %param.13) | copy-start | bytes 98308
  93.7 106.6 %all-gather.2.cloned.1.call-start = ((), (), s32[]{:S(2)}) async-start(), calls=%async_computation.3 | async-start | bytes 4718592 | tf_op jit(solution)/shard_map/all_gather | solution.py:122
  149.6 3.9 %copy-start.7 = (bf16[128,4]{0,1:T(4,128)(2,1)S(1)}, bf16[128,4]{0,1:T(4,128)(2,1)}, u32[]{:S(2)}) copy-start(bf16[128,4]{0,1:T(4,128)(2,1)} %param.16) | copy-start | bytes 3076
  165.3 11.0 %all-to-all-start = ((bf16[8,2,2048]{2,1,0:T(2,128)(2,1)}), bf16[8,2,2048]{2,1,0:T(2,128)(2,1)S(1)}, u32[]{:S(2)}, u32[]{:S(2)}) async-start(bf16[8,2,2048]{2,1,0:T(2,128)(2,1)} %reshape.132), calls=%async_computation.1 | async-start | bytes 131072 | tf_op jit(solution)/shard_map/all_to_all | solution.py:104
  204.9 3.5 %copy-start.5 = (f32[8,8,4,32]{3,2,1,0:T(4,128)S(1)}, f32[8,8,4,32]{3,2,1,0:T(4,128)}, u32[]{:S(2)}) copy-start(f32[8,8,4,32]{3,2,1,0:T(4,128)} %custom-call) | copy-start | bytes 98308
  252.6 2.9 %copy-start.3 = (bf16[64,32,128]{2,1,0:T(8,128)(2,1)S(1)}, bf16[64,32,128]{2,1,0:T(8,128)(2,1)}, u32[]{:S(2)}) copy-start(bf16[64,32,128]{2,1,0:T(8,128)(2,1)} %multiply_convert_fusion) | copy-start | bytes 1572868
  252.6 2.9 %copy-start.9 = (bf16[128,128]{1,0:T(8,128)(2,1)S(1)}, bf16[128,128]{1,0:T(8,128)(2,1)}, u32[]{:S(2)}) copy-start(bf16[128,128]{1,0:T(8,128)(2,1)} %param.17) | copy-start | bytes 98308
  252.6 5.2 %copy-start.1 = (bf16[128,512]{1,0:T(8,128)(2,1)S(1)}, bf16[128,512]{1,0:T(8,128)(2,1)}, u32[]{:S(2)}) copy-start(bf16[128,512]{1,0:T(8,128)(2,1)} %param.12) | copy-start | bytes 393220
Sparse Core Ops, SparseCore 0:
  93.9 50.4 reduce-scatter.1
  153.5 46.7 all-gather.1
